TPU v7x, 32 devices: a whole 2x2x4 slice. The times are simulated.
32 devices in a mesh: dp: 2 (over x), ep: 16 (over z, y, core).
Axes of the slice: x: 2, y: 2, z: 4, core: 2. Of those that a mesh axis runs over, the one named last changes fastest.
Arguments:
- tokens: bfloat16 [4096, 2048], P(('dp', 'ep')), parts along dimension 0
- expert_ids: int32 [4096, 8], P(('dp', 'ep')), parts along dimension 0
- norm_gain: bfloat16 [2048], replicated
- w_router: bfloat16 [2048, 128], replicated
- w_gate: bfloat16 [128, 2048, 768], P('ep')
- w_up: bfloat16 [128, 2048, 768], P('ep')
- w_down: bfloat16 [128, 768, 2048], P('ep')
Outputs:
- output: bfloat16 [4096, 2048], P(('dp', 'ep')), parts along dimension 0
There are 2 independent parts. A program takes and returns all parts, laid end to end along the dimension named above; an argument that names none is the same for every part.
All inputs are finite; a program needn't handle non-finite values.
Results may differ from a plain program's by a relative error of at most 0.00575139.
Values are sent between devices in bfloat16 or wider.
A program may use at most 1 GiB of HBM per device.

v0:
```python
import jax
import jax.numpy as jnp
from jax import lax
from jax.sharding import PartitionSpec as P

NORM_EPS = 1e-5


def rms_norm(tok_rows, norm_gain):
    tok32 = tok_rows.astype(jnp.float32)
    inv_rms = lax.rsqrt(jnp.mean(tok32 * tok32, axis=1, keepdims=True) + NORM_EPS)
    return (tok32 * inv_rms * norm_gain.astype(jnp.float32)).astype(jnp.bfloat16)


def expert_ffn(rows, w_gate, w_up, w_down, group_sizes):
    hidden_gate = lax.ragged_dot(rows, w_gate, group_sizes, preferred_element_type=jnp.float32)
    hidden_up = lax.ragged_dot(rows, w_up, group_sizes, preferred_element_type=jnp.float32)
    swiglu_out = (jax.nn.silu(hidden_gate) * hidden_up).astype(jnp.bfloat16)
    return lax.ragged_dot(swiglu_out, w_down, group_sizes, preferred_element_type=jnp.float32).astype(jnp.bfloat16)


def route_plan(expert_ids, ep_size, e_local, send_max):
    tok_count, top_k = expert_ids.shape
    pairs = tok_count * top_k
    flat_ids = expert_ids.reshape(pairs)
    sort_order = jnp.argsort(flat_ids, stable=True)
    sorted_dev = flat_ids[sort_order] // e_local
    expert_count = jnp.bincount(flat_ids, length=ep_size * e_local).astype(jnp.int32)
    dev_count = expert_count.reshape(ep_size, e_local).sum(axis=1)
    dev_start = jnp.cumsum(dev_count) - dev_count
    slot_sorted = sorted_dev * send_max + jnp.arange(pairs) - dev_start[sorted_dev]
    slot_of_pair = jnp.zeros((pairs,), jnp.int32).at[sort_order].set(slot_sorted)
    sorted_pos = jnp.minimum(dev_start[:, None] + jnp.arange(send_max)[None, :], pairs - 1)
    send_tok = (sort_order[sorted_pos] // top_k).reshape(ep_size * send_max)
    return expert_count.reshape(ep_size, e_local), slot_of_pair, send_tok


def recv_plan(recv_count, send_max, recv_max):
    ep_size, e_local = recv_count.shape
    row_end = jnp.cumsum(recv_count, axis=1)
    row_begin = row_end - recv_count
    slot_rank = jnp.arange(send_max)
    slot_expert = jnp.sum(row_end[:, None, :] <= slot_rank[None, :, None], axis=2)
    expert_safe = jnp.minimum(slot_expert, e_local - 1)
    expert_total = recv_count.sum(axis=0)
    expert_start = jnp.cumsum(expert_total) - expert_total
    src_before = jnp.cumsum(recv_count, axis=0) - recv_count
    offset = expert_start[None, :] + src_before - row_begin
    compact_pos = jnp.where(slot_expert < e_local, jnp.take_along_axis(offset, expert_safe, axis=1) + slot_rank[None, :], recv_max).reshape(ep_size * send_max)
    compact_src = jnp.zeros((recv_max,), jnp.int32).at[compact_pos].set(jnp.arange(ep_size * send_max), mode='drop')
    return expert_total, compact_src, jnp.minimum(compact_pos, recv_max - 1)


def solution(mesh):
    ep_size = mesh.shape['ep']

    def device_step(tokens, expert_ids, norm_gain, w_router, w_gate, w_up, w_down):
        tok_count, top_k = expert_ids.shape
        width = tokens.shape[1]
        e_local = w_gate.shape[0]
        pairs = tok_count * top_k
        send_max = 2 * pairs // ep_size
        recv_max = 3 * pairs // 2
        normed = rms_norm(tokens, norm_gain)
        router_prob = jax.nn.softmax(jnp.dot(normed, w_router, preferred_element_type=jnp.float32), axis=1)
        gate_vals = jnp.take_along_axis(router_prob, expert_ids, axis=1)
        send_count, slot_of_pair, send_tok = route_plan(expert_ids, ep_size, e_local, send_max)
        send_rows = normed[send_tok].reshape(ep_size, send_max, width)
        recv_count = lax.all_to_all(send_count, 'ep', 0, 0, tiled=True)
        recv_rows = lax.all_to_all(send_rows, 'ep', 0, 0, tiled=True)
        expert_total, compact_src, back_pos = recv_plan(recv_count, send_max, recv_max)
        compact_rows = recv_rows.reshape(ep_size * send_max, width)[compact_src]
        expert_out = expert_ffn(compact_rows, w_gate, w_up, w_down, expert_total)
        back_rows = expert_out[back_pos].reshape(ep_size, send_max, width)
        home_rows = lax.all_to_all(back_rows, 'ep', 0, 0, tiled=True)
        pair_out = home_rows.reshape(ep_size * send_max, width)[slot_of_pair].reshape(tok_count, top_k, width)
        moe_sum = jnp.sum(gate_vals[:, :, None] * pair_out, axis=1)
        return (tokens.astype(jnp.float32) + moe_sum).astype(jnp.bfloat16)

    row_spec = P(('dp', 'ep'), None)
    expert_spec = P('ep', None, None)
    return jax.shard_map(device_step, mesh=mesh, in_specs=(row_spec, row_spec, P(None), P(None, None), expert_spec, expert_spec, expert_spec), out_specs=row_spec, check_vma=False)
```

profile of v0, /device:TPU:13, one launch (start us, length us, event | category | flops | bytes accessed | tf_op | source)
XLA Modules:
  0.0 564.7 jit_solution(17900379136619085545)
XLA Ops:
  0.0 0.8 broadcast_maximum_fusion
  1.0 7.6 %scatter_custom_fusion = s32[128]{0:T(128)S(1)} fusion(s32[1024]{0:T(1024)S(1)} %reshape.517, s32[1024]{0:T(1024)S(1)} %broadcast.465, s32[]{:T(128)} %constant.50.clone.1), kind=kCustom, calls=%fused_computation.96 | custom fusion | flops 1024 | bytes 516 | tf_op jit(solution)/shard_map/scatter-add | solution.py:28
  9.3 6.5 %all-to-all-start.1 = ((s32[16,1,8]{2,1,0:T(1,128)}), s32[16,1,8]{2,1,0:T(1,128)S(1)}, u32[]{:S(2)}, u32[]{:S(2)}) async-start(s32[16,1,8]{2,1,0:T(1,128)} %bitcast.1), calls=%async_computation.1 | async-start | bytes 16384 | tf_op jit(solution)/shard_map/all_to_all | solution.py:69
  15.9 0.8 copy.61
  16.7 1.2 fusion.1
  19.2 4.4 sort.17
  23.5 8.6 %gather_fusion = s32[2048]{0:T(1024)S(1)} fusion(s32[1024]{0:T(1024)S(1)} %get-tuple-element.6, s32[2048]{0:T(1024)S(1)} %fusion.8), kind=kCustom, calls=%fused_computation | custom fusion | bytes 24576 | tf_op jit(solution)/shard_map/gather | solution.py:34
  32.4 11.0 %gather_fusion.1 = bf16[2048,2048]{1,0:T(8,128)(2,1)} fusion(bf16[128,2048]{1,0:T(8,128)(2,1)S(1)} %fusion.3, s32[2048]{0:T(1024)S(1)} %broadcast_clamp_fusion.1), kind=kCustom, calls=%fused_computation.1 | custom fusion | bytes 16785408 | tf_op jit(solution)/shard_map/gather | solution.py:68
  43.4 6.0 %all-to-all-start = ((bf16[16,128,2048]{2,1,0:T(8,128)(2,1)}), bf16[16,128,2048]{2,1,0:T(8,128)(2,1)}, u32[]{:S(2)}, u32[]{:S(2)}) async-start(bf16[16,128,2048]{2,1,0:T(8,128)(2,1)} %bitcast.68), calls=%async_computation | async-start | bytes 16777216 | tf_op jit(solution)/shard_map/all_to_all | solution.py:70
  50.2 1.5 ragged-dot-metadata
  51.7 0.8 reduce-window.16
  53.4 13.6 %gather_fusion.7 = s32[2048]{0:T(1024)S(1)} fusion(s32[16,8]{1,0:T(8,128)S(1)} %subtract_subtract_fusion, s32[2048]{0:T(1024)S(1)} %fusion.12), kind=kCustom, calls=%fused_computation.7 | custom fusion | bytes 32768 | tf_op jit(solution)/shard_map/jit(take_along_axis)/gather | solution.py:49
  67.1 8.0 %scatter_custom_fusion.1 = s32[1536]{0:T(1024)S(1)} fusion(s32[2048]{0:T(1024)S(1)} %bitcast.80, s32[2048]{0:T(1024)S(1)} %iota.22, s32[]{:T(128)} %constant.50.clone.1), kind=kCustom, calls=%fused_computation.86 | custom fusion | bytes 6148 | tf_op jit(solution)/shard_map/scatter | solution.py:50
  75.2 156.9 %all-to-all-done = bf16[16,128,2048]{2,1,0:T(8,128)(2,1)} async-done(((bf16[16,128,2048]{2,1,0:T(8,128)(2,1)}), bf16[16,128,2048]{2,1,0:T(8,128)(2,1)}, u32[]{:S(2)}, u32[]{:S(2)}) %all-to-all-start) | async-done | bytes 8388640 | tf_op jit(solution)/shard_map/all_to_all | solution.py:70
  232.1 17.1 %gather_fusion.2 = bf16[1536,2048]{1,0:T(8,128)(2,1)} fusion(bf16[2048,2048]{1,0:T(8,128)(2,1)} %bitcast.7, s32[2048]{0:T(1024)S(1)} %pad_clamp_fusion), kind=kCustom, calls=%fused_computation.2 | custom fusion | bytes 12589056 | tf_op jit(solution)/shard_map/gather | solution.py:72
  249.2 20.7 %ragged-dot-none.2 = f32[1536,768]{1,0:T(8,128)} custom-call(s32[1]{0:T(128)} %get-tuple-element.7, s32[9]{0:T(128)} %get-tuple-element.8, s32[13]{0:T(128)} %get-tuple-element.9, s32[13]{0:T(128)} %get-tuple-element.10, s32[1]{0:T(128)} %get-tuple-element.7, bf16[1536,2048]{1,0:T(8,128)(2,1)} %gather_fusion.2, bf16[8,2048,768]{2,1,0:T(8,128)(2,1)} %param.11), custom_call_target="tpu_custom_call" | custom-call | flops 4831838208 | bytes 36175904 | tf_op jit(solution)/shard_map/ragged_dot_general/ragged-dot-none
  269.9 20.7 %ragged-dot-none.1 = f32[1536,768]{1,0:T(8,128)} custom-call(s32[1]{0:T(128)} %get-tuple-element.7, s32[9]{0:T(128)} %get-tuple-element.8, s32[13]{0:T(128)} %get-tuple-element.9, s32[13]{0:T(128)} %get-tuple-element.10, s32[1]{0:T(128)} %get-tuple-element.7, bf16[1536,2048]{1,0:T(8,128)(2,1)} %gather_fusion.2, bf16[8,2048,768]{2,1,0:T(8,128)(2,1)} %param.12), custom_call_target="tpu_custom_call" | custom-call | flops 4831838208 | bytes 36175904 | tf_op jit(solution)/shard_map/ragged_dot_general/ragged-dot-none
  290.6 6.5 %multiply_convert_fusion = bf16[1536,768]{1,0:T(8,128)(2,1)} fusion(f32[1536,768]{1,0:T(8,128)} %ragged-dot-none.1, f32[1536,768]{1,0:T(8,128)} %ragged-dot-none.2), kind=kLoop, calls=%fused_computation.13 | loop fusion | flops 7077888 | bytes 11796480 | tf_op jit(solution)/shard_map/convert_element_type | solution.py:18
  297.1 22.4 %ragged-dot-none = f32[1536,2048]{1,0:T(8,128)} custom-call(s32[1]{0:T(128)} %get-tuple-element.7, s32[9]{0:T(128)} %get-tuple-element.8, s32[13]{0:T(128)} %get-tuple-element.9, s32[13]{0:T(128)} %get-tuple-element.10, s32[1]{0:T(128)} %get-tuple-element.7, bf16[1536,768]{1,0:T(8,128)(2,1)} %multiply_convert_fusion, bf16[8,768,2048]{2,1,0:T(8,128)(2,1)} %param.13), custom_call_target="tpu_custom_call" | custom-call | flops 4831838208 | bytes 40108064 | tf_op jit(solution)/shard_map/ragged_dot_general/ragged-dot-none
  319.5 8.2 %convert_element_type.33 = bf16[1536,2048]{1,0:T(8,128)(2,1)} convert(f32[1536,2048]{1,0:T(8,128)} %ragged-dot-none) | non-fusion elementwise | flops 3145728 | bytes 18874368 | tf_op jit(solution)/shard_map/convert_element_type | solution.py:19
  327.7 19.9 %gather_fusion.3 = bf16[2048,2048]{1,0:T(8,128)(2,1)} fusion(bf16[1536,2048]{1,0:T(8,128)(2,1)} %convert_element_type.33, s32[2048]{0:T(1024)S(1)} %broadcast_clamp_fusion), kind=kCustom, calls=%fused_computation.3 | custom fusion | bytes 16785408 | tf_op jit(solution)/shard_map/gather | solution.py:74
  347.6 13.7 %all-to-all-start.2 = ((bf16[16,128,2048]{2,1,0:T(8,128)(2,1)}), bf16[16,128,2048]{2,1,0:T(8,128)(2,1)}, u32[]{:S(2)}, u32[]{:S(2)}) async-start(bf16[16,128,2048]{2,1,0:T(8,128)(2,1)} %bitcast.67), calls=%async_computation.2 | async-start | bytes 16777216 | tf_op jit(solution)/shard_map/all_to_all | solution.py:75
  361.6 4.5 gather_fusion.4
  366.5 7.0 %gather_fusion.6 = f32[1024]{0:T(1024)S(1)} fusion(f32[128,128]{0,1:T(8,128)S(1)} %fusion.5, s32[1024]{0:T(1024)S(1)} %reshape.503), kind=kCustom, calls=%fused_computation.6 | custom fusion | bytes 16384 | tf_op jit(solution)/shard_map/jit(take_along_axis)/gather | solution.py:66
  373.8 0.7 fusion.26
  374.6 4.4 compare_select_fusion.11
  379.1 5.6 fusion.17
  384.7 4.5 scatter_custom_fusion.2
  389.2 154.7 %all-to-all-done.2 = bf16[16,128,2048]{2,1,0:T(8,128)(2,1)} async-done(((bf16[16,128,2048]{2,1,0:T(8,128)(2,1)}), bf16[16,128,2048]{2,1,0:T(8,128)(2,1)}, u32[]{:S(2)}, u32[]{:S(2)}) %all-to-all-start.2) | async-done | bytes 8388640 | tf_op jit(solution)/shard_map/all_to_all | solution.py:75
  543.9 13.3 %gather_fusion.5 = bf16[1024,2048]{1,0:T(8,128)(2,1)} fusion(bf16[2048,2048]{1,0:T(8,128)(2,1)} %bitcast.23, s32[1024]{0:T(1024)S(1)} %fusion.18), kind=kCustom, calls=%fused_computation.5 | custom fusion | bytes 8392704 | tf_op jit(solution)/shard_map/gather | solution.py:76
  557.2 6.5 %fusion = f32[128,2048]{1,0:T(8,128)S(1)} fusion(bf16[1024,2048]{1,0:T(8,128)(2,1)} %gather_fusion.5, f32[128,8]{1,0:T(8,128)S(1)} %copy.58), kind=kLoop, calls=%fused_computation.12 | loop fusion | flops 6029312 | bytes 5246976 | tf_op jit(solution)/shard_map/reduce_sum | solution.py:77
  563.8 0.9 fusion.4
  (54 shorter events, 5.1 us)
Async XLA Ops:
  0.0 366.1 %copy-start = (bf16[2048,128]{1,0:T(8,128)(2,1)S(1)}, bf16[2048,128]{1,0:T(8,128)(2,1)}, u32[]{:S(2)}) copy-start(bf16[2048,128]{1,0:T(8,128)(2,1)} %param.10) | copy-start | bytes 1572868
  0.0 32.2 %copy-start.1 = (bf16[128,2048]{1,0:T(8,128)(2,1)S(1)}, bf16[128,2048]{1,0:T(8,128)(2,1)}, u32[]{:S(2)}) copy-start(bf16[128,2048]{1,0:T(8,128)(2,1)} %param.7) | copy-start | bytes 1572868
  9.3 34.1 %all-to-all-start.1 = ((s32[16,1,8]{2,1,0:T(1,128)}), s32[16,1,8]{2,1,0:T(1,128)S(1)}, u32[]{:S(2)}, u32[]{:S(2)}) async-start(s32[16,1,8]{2,1,0:T(1,128)} %bitcast.1), calls=%async_computation.1 | async-start | bytes 16384 | tf_op jit(solution)/shard_map/all_to_all | solution.py:69
  43.4 188.6 %all-to-all-start = ((bf16[16,128,2048]{2,1,0:T(8,128)(2,1)}), bf16[16,128,2048]{2,1,0:T(8,128)(2,1)}, u32[]{:S(2)}, u32[]{:S(2)}) async-start(bf16[16,128,2048]{2,1,0:T(8,128)(2,1)} %bitcast.68), calls=%async_computation | async-start | bytes 16777216 | tf_op jit(solution)/shard_map/all_to_all | solution.py:70
  347.6 13.7 %copy-start.2 = (s32[128,8]{0,1:T(8,128)S(1)}, s32[128,8]{0,1:T(8,128)}, u32[]{:S(2)}) copy-start(s32[128,8]{0,1:T(8,128)} %param.8) | copy-start | bytes 12292
  347.6 196.3 %all-to-all-start.2 = ((bf16[16,128,2048]{2,1,0:T(8,128)(2,1)}), bf16[16,128,2048]{2,1,0:T(8,128)(2,1)}, u32[]{:S(2)}, u32[]{:S(2)}) async-start(bf16[16,128,2048]{2,1,0:T(8,128)(2,1)} %bitcast.67), calls=%async_computation.2 | async-start | bytes 16777216 | tf_op jit(solution)/shard_map/all_to_all | solution.py:75
where the time goes:
time: 567 us; the launch traced here: 565 us
  waiting for transfers between devices  312 us (55%)
  local copies, waits for them, and re-layouts  111 us (20%)
  Pallas kernels  65.3 us (12%)
  other arithmetic  50.1 us (9%)
  starting transfers between devices  26.2 us (5%)
    all_to_all x1, waiting for transfers between devices, device_step(): recv_rows = lax.all_to_all(send_rows, 'ep', 0, 0, tiled=True)  157 us
    all_to_all x1, waiting for transfers between devices, device_step(): home_rows = lax.all_to_all(back_rows, 'ep', 0, 0, tiled=True)  155 us
    another operation x3, Pallas kernels  63.8 us
    gather x1, local copies, waits for them, and re-layouts, device_step(): back_rows = expert_out[back_pos].reshape(ep_size, send_max, width)  19.9 us
    gather x1, local copies, waits for them, and re-layouts, device_step(): compact_rows = recv_rows.reshape(ep_size * send_max, width)[compact_src]  17.1 us
    all_to_all x1, starting transfers between devices, device_step(): home_rows = lax.all_to_all(back_rows, 'ep', 0, 0, tiled=True)  13.7 us
    gather x1, local copies, waits for them, and re-layouts, recv_plan(): jnp.take_along_axis(offset, expert_safe, axis=1) + slot_rank[None, :]  13.6 us
    gather x1, local copies, waits for them, and re-layouts, device_step(): home_rows.reshape(ep_size * send_max, width)[slot_of_pair]  13.3 us
  transfers between devices with their start and end apart: 3, of which 2 were waited for; matrix products, arithmetic and copies ran while one was open for 14% of the time, Pallas kernels for 0%

commit v1 on v0

v1 whole, which is shorter than its diff:
```python
import functools

import jax
import jax.numpy as jnp
from jax import lax
from jax.experimental import pallas as pl
from jax.experimental.pallas import tpu as pltpu
from jax.sharding import PartitionSpec as P

NORM_EPS = 1e-5
LANES = 128
BM = 256


def rms_norm(tok_rows, norm_gain):
    tok32 = tok_rows.astype(jnp.float32)
    inv_rms = lax.rsqrt(jnp.mean(tok32 * tok32, axis=1, keepdims=True) + NORM_EPS)
    return (tok32 * inv_rms * norm_gain.astype(jnp.float32)).astype(jnp.bfloat16)


def expert_kernel(n_src, sub, cnt, lst, gts, u_hbm, w1, w3, w2, out_hbm, u_vm, acc, xf, xb, hb, o3, sems):
    e = pl.program_id(0)
    n_exp = pl.num_programs(0)

    @pl.when(e == 0)
    def _():
        cp = pltpu.make_async_copy(u_hbm, u_vm, sems.at[0])
        cp.start()

        @pl.loop(0, acc.shape[0] // 256)
        def _(i):
            acc[pl.ds(pl.multiple_of(i * 256, 256), 256), :] = jnp.zeros((256, LANES), jnp.float32)

        cp.wait()

    def block(s0):
        def gather_src(carry):
            s, n = carry
            c = cnt[s, e]
            base = (s * n_exp + e) * LANES

            def row(i, _):
                t = s * LANES + lst[base + i]
                src = u_vm[pl.ds(pl.multiple_of(t * sub, sub), sub), :]
                xf[pl.ds(pl.multiple_of((n + i) * sub, sub), sub), :] = src.astype(jnp.float32)
                return 0

            lax.fori_loop(0, c, row, 0)
            return s + 1, n + c

        def fits(carry):
            s, n = carry
            return jnp.logical_and(s < n_src, n + cnt[jnp.minimum(s, n_src - 1), e] <= BM)

        s1, n_rows = lax.while_loop(fits, gather_src, (s0, jnp.int32(0)))

        @pl.when(n_rows > 0)
        def _():
            for j in range(sub):
                xb[:, j * LANES:(j + 1) * LANES] = xf[pl.ds(j, BM, stride=sub), :].astype(jnp.bfloat16)
            g = jnp.dot(xb[...], w1[0], preferred_element_type=jnp.float32)
            v = jnp.dot(xb[...], w3[0], preferred_element_type=jnp.float32)
            hb[...] = (jax.nn.silu(g) * v).astype(jnp.bfloat16)
            for q in range(sub // 4):
                o = jnp.dot(hb[...], w2[0, :, q * 512:(q + 1) * 512], preferred_element_type=jnp.float32)
                o = o.astype(jnp.bfloat16).astype(jnp.float32)
                for j in range(4):
                    o3[pl.ds(q * 4 + j, BM, stride=sub), :] = o[:, j * LANES:(j + 1) * LANES]

            def scatter_src(s, n):
                c = cnt[s, e]
                base = (s * n_exp + e) * LANES

                def row(i, _):
                    t = s * LANES + lst[base + i]
                    ts = pl.ds(pl.multiple_of(t * sub, sub), sub)
                    acc[ts, :] += gts[base + i] * o3[pl.ds(pl.multiple_of((n + i) * sub, sub), sub), :]
                    return 0

                lax.fori_loop(0, c, row, 0)
                return n + c

            lax.fori_loop(s0, s1, scatter_src, jnp.int32(0))

        return s1

    lax.while_loop(lambda s: s < n_src, block, jnp.int32(0))

    @pl.when(e == n_exp - 1)
    def _():
        cp = pltpu.make_async_copy(acc, out_hbm, sems.at[0])
        cp.start()
        cp.wait()


def experts(n_src, cnt, lst, gts, u_rows, w1, w3, w2):
    n_exp, width, ff = w1.shape
    sub = width // LANES
    n_tok = u_rows.shape[0] // sub
    any_spec = pl.BlockSpec(memory_space=pl.ANY)
    smem = pl.BlockSpec(memory_space=pltpu.SMEM)
    return pl.pallas_call(
        functools.partial(expert_kernel, n_src, sub),
        grid=(n_exp,),
        out_shape=jax.ShapeDtypeStruct((n_tok * sub, LANES), jnp.float32),
        in_specs=[smem, smem, smem, any_spec,
                  pl.BlockSpec((1, width, ff), lambda e: (e, 0, 0)),
                  pl.BlockSpec((1, width, ff), lambda e: (e, 0, 0)),
                  pl.BlockSpec((1, ff, width), lambda e: (e, 0, 0))],
        out_specs=any_spec,
        scratch_shapes=[
            pltpu.VMEM((n_tok * sub, LANES), jnp.bfloat16),
            pltpu.VMEM((n_tok * sub, LANES), jnp.float32),
            pltpu.VMEM((BM * sub, LANES), jnp.float32),
            pltpu.VMEM((BM, width), jnp.bfloat16),
            pltpu.VMEM((BM, ff), jnp.bfloat16),
            pltpu.VMEM((BM * sub, LANES), jnp.float32),
            pltpu.SemaphoreType.DMA((1,)),
        ],
        compiler_params=pltpu.CompilerParams(vmem_limit_bytes=66_000_000, dimension_semantics=("arbitrary",)),
        name="experts",
    )(cnt, lst, gts, u_rows, w1, w3, w2)


def route_lists(expert_ids, router_prob, n_all):
    n_tok = expert_ids.shape[0]
    hit = jnp.any(expert_ids[:, :, None] == jnp.arange(n_all)[None, None, :], axis=1)
    hit_b = hit.astype(jnp.bfloat16)
    tri = (jnp.arange(n_tok)[:, None] > jnp.arange(n_tok)[None, :]).astype(jnp.bfloat16)
    pos = jnp.dot(tri, hit_b, preferred_element_type=jnp.float32).astype(jnp.int32)
    pos = jnp.where(hit, pos, n_tok)
    sel = pos[:, :, None] == jnp.arange(n_tok)[None, None, :]
    tok = jnp.sum(jnp.where(sel, jnp.arange(n_tok, dtype=jnp.float32)[:, None, None], 0.0), axis=0)
    gate = jnp.sum(jnp.where(sel, router_prob[:, :, None], 0.0), axis=0)
    count = jnp.sum(hit.astype(jnp.float32), axis=0)
    return count, tok, gate


def solution(mesh):
    ep_size = mesh.shape['ep']

    def device_step(tokens, expert_ids, norm_gain, w_router, w_gate, w_up, w_down):
        tok_count, width = tokens.shape
        e_local = w_gate.shape[0]
        n_all = ep_size * e_local
        sub = width // LANES
        normed = rms_norm(tokens, norm_gain)
        u_rows = lax.all_gather(normed.reshape(tok_count * sub, LANES), 'ep', axis=0, tiled=True)
        router_prob = jax.nn.softmax(jnp.dot(normed, w_router, preferred_element_type=jnp.float32), axis=1)
        count, tok, gate = route_lists(expert_ids, router_prob, n_all)
        meta = jnp.concatenate([tok.reshape(ep_size, e_local, LANES), gate.reshape(ep_size, e_local, LANES),
                                jnp.broadcast_to(count.reshape(ep_size, e_local, 1), (ep_size, e_local, LANES))], axis=1)
        meta = lax.all_to_all(meta, 'ep', 0, 0, tiled=True)
        lst = meta[:, :e_local].astype(jnp.int32).reshape(-1)
        gts = meta[:, e_local:2 * e_local].reshape(-1)
        cnt = meta[:, 2 * e_local:, 0].astype(jnp.int32)
        part = experts(ep_size, cnt, lst, gts, u_rows, w_gate, w_up, w_down)
        moe_sum = lax.psum_scatter(part, 'ep', scatter_dimension=0, tiled=True)
        return (tokens.astype(jnp.float32) + moe_sum.reshape(tok_count, width)).astype(jnp.bfloat16)

    row_spec = P(('dp', 'ep'), None)
    expert_spec = P('ep', None, None)
    return jax.shard_map(device_step, mesh=mesh, in_specs=(row_spec, row_spec, P(None), P(None, None), expert_spec, expert_spec, expert_spec), out_specs=row_spec, check_vma=False)
```

time: 567 us -> 347 us (0.61)
  the two profiles are of different devices: /device:TPU:13 before, /device:TPU:0 now
where the time goes in v1:
time: 347 us; the launch traced here: 346 us
  waiting for transfers between devices  235 us (68%)
  Pallas kernels  62.8 us (18%)
  blocking collectives  19.7 us (6%)
  between operations  13.5 us (4%)
  other arithmetic  10.8 us (3%)
  local copies, waits for them, and re-layouts  4.28 us (1%)
    reduce_scatter x1, waiting for transfers between devices, device_step(): moe_sum = lax.psum_scatter(part, 'ep', scatter_dimension=0, tiled=True)  182 us
    pallas_call x1, Pallas kernels, experts(): pl.pallas_call(functools.partial(expert_kernel, n_src, sub), grid=(n_exp,...  62.8 us
    all_gather x1, waiting for transfers between devices, device_step(): lax.all_gather(normed.reshape(tok_count * sub, LANES), 'ep', axis=0, tile...  52.7 us
    all_to_all x1, blocking collectives, device_step(): meta = lax.all_to_all(meta, 'ep', 0, 0, tiled=True)  19.7 us
  transfers between devices with their start and end apart: 2, of which 2 were waited for; matrix products, arithmetic and copies ran while one was open for 3% of the time, Pallas kernels for 0%

profile of v1, /device:TPU:0, one launch (start us, length us, event | category | flops | bytes accessed | tf_op | source)
XLA Modules:
  0.0 346.3 jit_solution(11439728532835751529)
XLA Ops:
  6.5 0.0 copy-start
  6.5 0.0 all-gather.2.cloned.1.call-start
  6.5 1.3 fusion.1
  7.8 0.7 convert_element_type.31
  8.5 1.2 fusion.3
  9.8 1.0 reshape.39
  10.8 0.0 all-gather.2.cloned.1.call-update
  10.8 0.0 reduce-scatter.2.cloned.1.call-start
  10.9 0.8 copy.28
  11.7 0.3 fusion.5
  12.0 0.1 broadcast_in_dim.49
  12.0 0.0 copy-done
  12.1 0.4 fusion.9
  12.5 0.1 copy.29
  12.6 0.1 fusion
  12.7 5.7 %select_reduce_fusion.1 = (f32[128,128]{1,0:T(8,128)S(1)}, f32[128,128]{1,0:T(8,128)S(1)}) fusion(s32[128,128]{1,0:T(8,128)S(1)} %fusion, f32[128,128]{1,0:T(8,128)S(1)} %copy.29), kind=kLoop, calls=%fused_computation.1 | loop fusion | flops 10452992 | bytes 262144 | tf_op jit(solution)/shard_map/reduce_sum | solution.py:133
  18.4 0.1 broadcast_in_dim.50
  18.5 19.7 %all_to_all.5 = f32[16,24,128]{2,1,0:T(8,128)S(1)} all-to-all(f32[16,24,128]{2,1,0:T(8,128)S(1)} %pad_maximum_fusion), channel_id=1, replica_groups=mesh['dp'=2,'ep'=16] {'ep'}, dimensions={0} | all-to-all | bytes 393216 | tf_op jit(solution)/shard_map/all_to_all | solution.py:153
  38.3 0.1 copy.32
  38.4 0.7 copy.31.cnt
  39.1 0.7 slice_bitcast_fusion
  39.7 52.7 %all-gather.2.cloned.1.call-done.u_hbm = bf16[32768,128]{1,0:T(8,128)(2,1)} async-done(((bf16[2048,128]{1,0:T(8,128)(2,1)}), bf16[32768,128]{1,0:T(8,128)(2,1)}) %all-gather.2.cloned.1.call-update) | async-done | bytes 8388624 | tf_op jit(solution)/shard_map/all_gather | solution.py:148
  92.4 62.8 %experts.1 = f32[32768,128]{1,0:T(8,128)} custom-call(s32[16,8]{1,0:T(8,128)} %copy.31.cnt, s32[16384]{0:T(1024)} %get-tuple-element.8.lst, f32[16384]{0:T(1024)} %get-tuple-element.7.gts, bf16[32768,128]{1,0:T(8,128)(2,1)} %all-gather.2.cloned.1.call-done.u_hbm, bf16[8,2048,768]{2,1,0:T(8,128)(2,1)} %w1.1, bf16[8,2048,768]{2,1,0:T(8,128)(2,1)} %w3.1, ...), custom_call_target="tpu_custom_call" | custom-call | tf_op jit(solution)/shard_map/experts/pallas_call | solution.py:102
  155.2 0.0 copy-start.1
  155.2 0.0 copy-start.2
  155.2 0.0 reduce-scatter.2.cloned.1.call-update
  155.3 181.9 %reduce-scatter.2.cloned.1.call-done = f32[2048,128]{1,0:T(8,128)} async-done(((f32[32768,128]{1,0:T(8,128)}), f32[2048,128]{1,0:T(8,128)}) %reduce-scatter.2.cloned.1.call-update) | async-done | bytes 1048592 | tf_op jit(solution)/shard_map/reduce_scatter | solution.py:158
  337.1 1.4 reshape.40
  338.5 0.0 copy-done.2
  338.5 0.9 fusion.4
  339.4 0.0 copy-done.1
  (7 shorter events, 0.1 us)
Async XLA Ops:
  6.5 5.5 %copy-start = (bf16[2048,128]{1,0:T(8,128)(2,1)S(1)}, bf16[2048,128]{1,0:T(8,128)(2,1)}, u32[]{:S(2)}) copy-start(bf16[2048,128]{1,0:T(8,128)(2,1)} %param.10) | copy-start | bytes 1572868
  6.5 85.9 %all-gather.2.cloned.1.call-start = ((), (), s32[]{:S(2)}) async-start(), calls=%async_computation.2 | async-start | bytes 8912896 | tf_op jit(solution)/shard_map/all_gather | solution.py:148
  10.8 326.3 %reduce-scatter.2.cloned.1.call-start = ((), (), s32[]{:S(2)}) async-start(), calls=%async_computation.3 | async-start | bytes 17825792 | tf_op jit(solution)/shard_map/reduce_scatter | solution.py:158
  155.2 184.2 %copy-start.1 = (bf16[2048,128]{1,0:T(8,128)(2,1)S(1)}, bf16[2048,128]{1,0:T(8,128)(2,1)}, u32[]{:S(2)}) copy-start(bf16[2048,128]{1,0:T(8,128)(2,1)} %param.10) | copy-start | bytes 1572868
  155.2 183.3 %copy-start.2 = (bf16[128,2048]{1,0:T(8,128)(2,1)S(1)}, bf16[128,2048]{1,0:T(8,128)(2,1)}, u32[]{:S(2)}) copy-start(bf16[128,2048]{1,0:T(8,128)(2,1)} %param.7) | copy-start | bytes 1572868
Sparse Core Ops, SparseCore 0:
  10.9 81.4 all-gather.1
  155.4 181.7 reduce-scatter.1
